TPU v7x, 512 devices: a whole 4x8x8 slice. The times are simulated.
512 devices in a mesh: rep: 8 (over x, y_hi), amp: 64 (over y_lo, z, core).
Axes of the slice: x: 4, y: 8 (y_hi: 2, y_lo: 4; y = y_hi * 4 + y_lo), z: 8, core: 2. Of those that a mesh axis runs over, the one named last changes fastest.
Arguments:
- amplitudes: float32 [2, 16777216], P(None, ('rep', 'amp')), parts along dimension 1, may hold values from -12 to 12
- coupling_index: int32 [16, 20], P('rep'), parts along dimension 0, may hold values from 0 to 15
- rotation_index: int32 [16, 21], P('rep'), parts along dimension 0, may hold values from 0 to 15
- chain_order: int32 [21], replicated, may hold values from 0 to 20, each once
- bond_sign: int32 [20], replicated, may hold values 0 or 1
Outputs:
- final_state: float32 [2, 16777216], P(None, ('rep', 'amp')), parts along dimension 1
- energies: float32 [16], P('rep'), parts along dimension 0
There are 8 independent parts, one for each index of `rep`. A program takes and returns all parts, laid end to end along the dimension named above; an argument that names none is the same for every part. Nothing has to cross between parts.
Inputs may be any that keep to these rules, and one draw needn't show every extreme that they name: chain_order holds each of 0 to 20 once.
All inputs are finite; a program needn't handle non-finite values.
Results may differ from a plain program's by a relative error of at most 0.0003.
Values sent between devices are 32-bit elements; how exact they have to be, the bound alone decides.
No kernel may reach another device: no remote copies, remote signals or barrier semaphores. Data moves between devices by JAX's collectives and lax.ppermute only.
A program may use at most 128 MiB of HBM per device.

v0:
```python
import numpy as np
import jax
import jax.numpy as jnp
from jax import lax
from jax.experimental import pallas as pl
from jax.experimental.pallas import tpu as pltpu
from jax.sharding import PartitionSpec as P

LAYERS = 2
ANGLES = 16
UNITS = 2 * (ANGLES + 1)
LANE_BITS = 7
LANES = 128

F32 = jnp.float32
BF16 = jnp.bfloat16


def angle_tables():
    steps = (np.arange(ANGLES, dtype=np.float64) + 1.0) * (np.pi / UNITS)
    return np.stack([np.cos(steps), np.sin(steps)]).astype(np.float32)


def iota(shape, dimension):
    return lax.broadcasted_iota(jnp.int32, shape, dimension)


def bit_count(values, width):
    total = values & 1
    for bit in range(1, width):
        total = total + ((values >> bit) & 1)
    return total


def split(values):
    high = values.astype(BF16)
    return high, (values - high.astype(F32)).astype(BF16)


def dot(left, right):
    return jnp.dot(left, right, preferred_element_type=F32)


def product(left, right):
    return dot(left[0], right[0]) + (dot(left[0], right[1]) + dot(left[1], right[0]))


def rotation(size, first, pairs):
    row, column = iota((size, size), 0), iota((size, size), 1)
    differ = row ^ column
    matrix = None
    for at, (cosine, sine) in enumerate(pairs):
        bit = first + at
        here = (differ >> bit) & 1
        low = jnp.where(((row >> bit) & 1) == 1, -sine, sine)
        factor = jnp.where(here == 1, low, cosine)
        matrix = factor if matrix is None else matrix * factor
    if first:
        matrix = jnp.where((differ & (2**first - 1)) == 0, matrix, 0.0)
    return matrix


def row_rotation(bits, first, pairs):
    half = rotation(2 ** (bits - 1), first, pairs[:-1])
    cosine, sine = pairs[-1]
    return jnp.concatenate(
        [
            jnp.concatenate([cosine * half, sine * half], axis=1),
            jnp.concatenate([-sine * half, cosine * half], axis=1),
        ],
        axis=0,
    )


def pair_of(layer, rotation_ref, table_ref, qubit):
    index = rotation_ref[layer, qubit]
    return table_ref[0, index], table_ref[1, index]


def signs(index, chain_ref, bonds):
    first, second = chain_ref[:, 0:bonds], chain_ref[:, 1 : bonds + 1]
    differ = (index >> first) ^ (index >> second)
    return (1 - 2 * (differ & 1)).astype(F32)


def fields(weights, index_rows, chain_ref, bonds):
    row_signs = signs(index_rows, chain_ref, bonds)
    lane_signs = signs(iota((LANES, bonds), 0), chain_ref, bonds).astype(BF16)
    rows = index_rows.shape[0]
    stacked = jnp.concatenate([(w * row_signs).astype(BF16) for w in weights], axis=0)
    out = lax.dot_general(
        stacked, lane_signs, (((1,), (1,)), ((), ())), preferred_element_type=F32
    )
    return [out[k * rows : (k + 1) * rows] for k in range(len(weights))]


def cos_sin(steps):
    quarter = UNITS // 2
    turns = jnp.floor(steps * (1.0 / quarter) + 0.5)
    angle = (steps - turns * quarter) * (np.pi / UNITS)
    square = angle * angle
    sine = angle * (
        1.0 + square * (-1.0 / 6 + square * (1.0 / 120 + square * (-1.0 / 5040 + square * (1.0 / 362880))))
    )
    cosine = 1.0 + square * (
        -0.5 + square * (1.0 / 24 + square * (-1.0 / 720 + square * (1.0 / 40320)))
    )
    turns = turns.astype(jnp.int32)
    odd = (turns & 1) == 1
    cosine, sine = jnp.where(odd, sine, cosine), jnp.where(odd, cosine, sine)
    return (
        jnp.where(((turns + 1) & 2) == 2, -cosine, cosine),
        jnp.where((turns & 2) == 2, -sine, sine),
    )


def evens(ref):
    half = ref.shape[0] // 2
    return ref[pl.ds(0, half, stride=2), :], ref[pl.ds(1, half, stride=2), :]


def put(ref, real, imag):
    half = ref.shape[0] // 2
    ref[pl.ds(0, half, stride=2), :] = real
    ref[pl.ds(1, half, stride=2), :] = imag


def by_rows(gate, real, imag):
    both = product(gate, split(jnp.concatenate([real, imag], axis=1)))
    return both[:, :LANES], both[:, LANES:]


def by_lanes(gate, real, imag):
    rows = real.shape[0]
    both = product(split(jnp.concatenate([real, imag], axis=0)), gate)
    return both[:rows], both[rows:]


class Plan:
    def __init__(self, local_bits, global_bits):
        self.local_bits, self.global_bits = local_bits, global_bits
        self.qubits = local_bits + global_bits
        self.rows = 2 ** (local_bits - LANE_BITS)
        self.row_bits = local_bits - LANE_BITS
        self.kept = self.row_bits - global_bits
        self.bonds = self.qubits - 1

    def rows_plain(self, device, bonds):
        return (iota((self.rows, bonds), 0) << LANE_BITS) | (device << self.local_bits)

    def rows_moved(self, device, bonds):
        row = iota((self.rows, bonds), 0)
        low = (row & (2**self.kept - 1)) << LANE_BITS
        return low | ((row >> self.kept) << self.local_bits) | (device << (LANE_BITS + self.kept))

    def row_qubits(self, moved):
        low = [LANE_BITS + k for k in range(self.kept)]
        start = self.local_bits if moved else LANE_BITS + self.kept
        return low + [start + k for k in range(self.global_bits)]


def first_kernel(plan, rotation_ref, table_ref, chain_ref, coupling_ref, bond_ref, amps_ref, out_ref, norm_ref):
    device = lax.axis_index("amp")
    bonds = plan.bonds
    bond_signs = (2 * bond_ref[...] - 1).astype(F32)
    weight = (coupling_ref[0:1, :] + 1).astype(F32) * bond_signs
    (steps,) = fields([weight], plan.rows_plain(device, bonds), chain_ref, bonds)
    ones = bit_count(iota((plan.rows, LANES), 0), plan.row_bits) + bit_count(
        iota((plan.rows, LANES), 1), LANE_BITS
    )
    ones = ones + bit_count(device, plan.global_bits)
    steps = steps + (UNITS // 2) * ones.astype(F32)
    cosine, sine = cos_sin(steps)
    pairs = lambda qs: [pair_of(0, rotation_ref, table_ref, q) for q in qs]
    row_gate = split(row_rotation(plan.row_bits, 0, pairs(plan.row_qubits(False))))
    lane_gate = split(rotation(LANES, 0, [(c, -s) for c, s in pairs(range(LANE_BITS))]))
    real, imag = evens(amps_ref)
    norm_ref[...] = jnp.sum((real * real + imag * imag).reshape(-1, 8, LANES), axis=0)
    real, imag = cosine * real + sine * imag, cosine * imag - sine * real
    real, imag = by_lanes(lane_gate, *by_rows(row_gate, real, imag))
    put(out_ref, real, imag)


def prepare_kernel(
    plan, rotation_ref, table_ref, chain_ref, coupling_ref, bond_ref,
    cosine_ref, sine_ref, moved_ref, plain_ref, *gate_refs,
):
    device = lax.axis_index("amp")
    bonds = plan.bonds
    bond_signs = (2 * bond_ref[...] - 1).astype(F32)
    weight = (coupling_ref[1:2, :] + 1).astype(F32) * bond_signs
    steps, moved = fields([weight, bond_signs], plan.rows_moved(device, bonds), chain_ref, bonds)
    cosine_ref[...], sine_ref[...] = cos_sin(steps)
    moved_ref[...] = moved
    (plain_ref[...],) = fields([bond_signs], plan.rows_plain(device, bonds), chain_ref, bonds)
    pairs = lambda layer, qs: [pair_of(layer, rotation_ref, table_ref, q) for q in qs]
    kept = plan.kept
    gates = [
        row_rotation(plan.row_bits, kept, pairs(0, plan.row_qubits(True)[kept:])),
        row_rotation(plan.row_bits, 0, pairs(1, plan.row_qubits(True))),
        rotation(LANES, 0, [(c, -s) for c, s in pairs(1, range(LANE_BITS))]),
        row_rotation(plan.row_bits, kept, pairs(1, plan.row_qubits(False)[kept:])),
    ]
    for k, gate in enumerate(gates):
        gate_refs[2 * k][...], gate_refs[2 * k + 1][...] = split(gate)


def energy(real, imag, field):
    return jnp.sum(((real * real + imag * imag) * field).reshape(-1, 8, LANES), axis=0)


def middle_kernel(state_ref, cosine_ref, sine_ref, moved_ref, *refs):
    (ga, gb, ha, hb, la, lb), (out_ref, energy_ref) = refs[:6], refs[6:]
    real, imag = by_rows((ga[...], gb[...]), *evens(state_ref))
    energy_ref[...] = energy(real, imag, moved_ref[...])
    cosine, sine = cosine_ref[...], sine_ref[...]
    real, imag = cosine * real + sine * imag, cosine * imag - sine * real
    real, imag = by_rows((ha[...], hb[...]), real, imag)
    real, imag = by_lanes((la[...], lb[...]), real, imag)
    put(out_ref, real, imag)


def last_kernel(plan, state_ref, plain_ref, ga, gb, norm_ref, energy_ref, out_ref, sums_ref):
    device = lax.axis_index("amp")
    real, imag = by_rows((ga[...], gb[...]), *evens(state_ref))
    second = energy(real, imag, plain_ref[...])
    lane = iota((1, LANES), 1)
    sums = jnp.zeros((1, LANES), F32)
    for k, part in enumerate((norm_ref[...], energy_ref[...], second)):
        sums = jnp.where(lane == k, jnp.sum(part), sums)
    sums_ref[...] = jnp.broadcast_to(sums[None], sums_ref.shape)
    ones = bit_count(iota((plan.rows, LANES), 0), plan.row_bits) + bit_count(
        iota((plan.rows, LANES), 1), LANE_BITS
    )
    ones = ones + bit_count(device, plan.global_bits)
    odd = (ones & 1) == 1
    real, imag = jnp.where(odd, imag, real), jnp.where(odd, real, imag)
    put(
        out_ref,
        jnp.where(((ones + 1) & 2) == 2, -real, real),
        jnp.where((ones & 2) == 2, -imag, imag),
    )


def finish_kernel(plan, state_ref, sums_ref, out_ref, energies_ref):
    total = jnp.sum(sums_ref[...], axis=0)
    amps = float(2**plan.qubits)
    square = 1.0 / (total[:, 0:1] / amps + 1e-06)
    out_ref[...] = state_ref[...] * lax.rsqrt(total[:, 0:1] / amps + 1e-06)
    energies_ref[...] = total[:, 1 : 1 + LAYERS] * square / amps


def spec(space):
    return pl.BlockSpec(memory_space=space)


def call(kernel, shapes, scalars, arrays, name):
    return pl.pallas_call(
        kernel,
        out_shape=shapes,
        in_specs=[spec(pltpu.SMEM)] * len(scalars) + [spec(pltpu.VMEM)] * len(arrays),
        out_specs=jax.tree.map(lambda _: spec(pltpu.VMEM), shapes),
        name=name,
    )(*scalars, *arrays)


def local(amplitudes, coupling_index, rotation_index, chain_order, bond_sign):
    local_bits = amplitudes.shape[1].bit_length() - 1
    size = lax.axis_size("amp")
    plan = Plan(local_bits, size.bit_length() - 1)
    rows = plan.rows
    shape = jax.ShapeDtypeStruct
    bind = lambda kernel: lambda *refs: kernel(plan, *refs)

    state = amplitudes.reshape(2, rows, LANES).transpose(1, 0, 2).reshape(2 * rows, LANES)
    table = jnp.asarray(angle_tables())
    chain, bond = chain_order.reshape(1, -1), bond_sign.reshape(1, -1)
    scalars = (rotation_index, table)
    small = (chain, coupling_index, bond)
    whole = shape((2 * rows, LANES), F32)
    part = shape((8, LANES), F32)
    field = shape((rows, LANES), F32)
    row_gate = shape((rows, rows), BF16)
    lane_gate = shape((LANES, LANES), BF16)

    def trade(array):
        blocks = array.reshape(size, 2 * rows // size, LANES)
        return lax.all_to_all(blocks, "amp", 0, 0, tiled=True).reshape(2 * rows, LANES)

    state, norm = call(bind(first_kernel), (whole, part), scalars, (*small, state), "first")
    cosine, sine, moved, plain, *gates = call(
        bind(prepare_kernel),
        (field, field, field, field, row_gate, row_gate, row_gate, row_gate, lane_gate, lane_gate, row_gate, row_gate),
        scalars, small, "prepare",
    )
    state = trade(state)
    state, first_energy = call(middle_kernel, (whole, part), (), (state, cosine, sine, moved, *gates[:6]), "middle")
    state = trade(state)
    state, sums = call(
        bind(last_kernel), (whole, shape((size, 1, LANES), F32)), (),
        (state, plain, *gates[6:], norm, first_energy), "last",
    )
    sums = lax.all_to_all(sums, "amp", 0, 0, tiled=True)
    state, energies = call(bind(finish_kernel), (whole, shape((1, LAYERS), F32)), (), (state, sums), "finish")
    final = state.reshape(rows, 2, LANES).transpose(1, 0, 2).reshape(2, rows * LANES)
    return final, energies.reshape(LAYERS)


def solution(mesh):
    in_specs = (P(None, ("rep", "amp")), P("rep", None), P("rep", None), P(), P())
    out_specs = (P(None, ("rep", "amp")), P("rep"))
    return jax.shard_map(local, mesh=mesh, in_specs=in_specs, out_specs=out_specs, check_vma=False)
```

profile of v0, /device:TPU:1, one launch (start us, length us, event | category | flops | bytes accessed | tf_op | source)
XLA Modules:
  0.0 71.7 jit_solution(15866817591360150240)
XLA Ops:
  0.6 3.0 %first.1 = (f32[512,128]{1,0:T(8,128)}, f32[8,128]{1,0:T(8,128)}) custom-call(s32[2,21]{1,0:T(2,128)} %refs_0_.3, f32[2,16]{1,0:T(2,128)} %constant.2.clone.refs_1_, s32[1,21]{1,0:T(1,128)} %bitcast.22, s32[2,20]{1,0:T(2,128)} %refs_3_.3, s32[1,20]{1,0:T(1,128)} %bitcast.24, f32[512,128]{1,0:T(8,128)} %bitcast.19), custom_call_target="tpu_custom_call" | custom-call | tf_op jit(solution)/shard_map/first/pallas_call | solution.py:258
  3.7 15.4 %all-to-all-start = ((f32[64,8,128]{2,1,0:T(8,128)}), f32[64,8,128]{2,1,0:T(8,128)S(1)}, u32[]{:S(2)}, u32[]{:S(2)}) async-start(f32[64,8,128]{2,1,0:T(8,128)} %bitcast.20), calls=%async_computation | async-start | bytes 524288 | tf_op jit(solution)/shard_map/all_to_all | solution.py:288
  19.1 2.5 %prepare.1 = (f32[256,128]{1,0:T(8,128)}, f32[256,128]{1,0:T(8,128)}, f32[256,128]{1,0:T(8,128)}, f32[256,128]{1,0:T(8,128)}, bf16[256,256]{1,0:T(8,128)(2,1)}, ...) custom-call(s32[2,21]{1,0:T(2,128)} %refs_0_.3, ...), custom_call_target="tpu_custom_call" | custom-call | tf_op jit(solution)/shard_map/prepare/pallas_call | solution.py:258
  21.6 9.0 %all-to-all-done = f32[64,8,128]{2,1,0:T(8,128)S(1)} async-done(((f32[64,8,128]{2,1,0:T(8,128)}), f32[64,8,128]{2,1,0:T(8,128)S(1)}, u32[]{:S(2)}, u32[]{:S(2)}) %all-to-all-start) | async-done | bytes 262176 | tf_op jit(solution)/shard_map/all_to_all | solution.py:288
  30.6 0.0 copy-start
  30.6 0.7 copy-done
  31.3 2.9 %middle.1 = (f32[512,128]{1,0:T(8,128)}, f32[8,128]{1,0:T(8,128)}) custom-call(f32[512,128]{1,0:T(8,128)} %bitcast.17, f32[256,128]{1,0:T(8,128)} %get-tuple-element.23.cosine_ref, f32[256,128]{1,0:T(8,128)} %get-tuple-element.24.sine_ref, f32[256,128]{1,0:T(8,128)} %get-tuple-element.25.moved_ref, bf16[256,256]{1,0:T(8,128)(2,1)} %get-tuple-element.26.refs_0_, ...), custom_call_target="tpu_custom_call" | custom-call | tf_op jit(solution)/shard_map/middle/pallas_call | solution.py:258
  34.2 17.8 %all_to_all.15 = f32[64,8,128]{2,1,0:T(8,128)} all-to-all(f32[64,8,128]{2,1,0:T(8,128)} %bitcast.21), channel_id=1, replica_groups=mesh['rep'=8,'amp'=64] {'amp'}, dimensions={0} | all-to-all | bytes 524288 | tf_op jit(solution)/shard_map/all_to_all | solution.py:288
  52.0 2.2 %last.1 = (f32[512,128]{1,0:T(8,128)}, f32[64,1,128]{2,1,0:T(1,128)}) custom-call(f32[512,128]{1,0:T(8,128)} %bitcast.18, f32[256,128]{1,0:T(8,128)} %get-tuple-element.33.refs_1_, bf16[256,256]{1,0:T(8,128)(2,1)} %get-tuple-element.34.refs_2_, bf16[256,256]{1,0:T(8,128)(2,1)} %get-tuple-element.35.refs_3_, f32[8,128]{1,0:T(8,128)} %get-tuple-element.36.refs_4_, ...), custom_call_target="tpu_custom_call" | custom-call | tf_op jit(solution)/shard_map/last/pallas_call | solution.py:258
  54.2 15.7 %all_to_all.16.refs_1_ = f32[64,1,128]{2,1,0:T(1,128)} all-to-all(f32[64,1,128]{2,1,0:T(1,128)} %get-tuple-element.39), channel_id=1, replica_groups=mesh['rep'=8,'amp'=64] {'amp'}, dimensions={0} | all-to-all | bytes 65536 | tf_op jit(solution)/shard_map/all_to_all | solution.py:303
  69.9 1.8 %finish.1 = (f32[512,128]{1,0:T(8,128)}, f32[1,2]{1,0:T(1,128)}) custom-call(f32[512,128]{1,0:T(8,128)} %get-tuple-element.38.refs_0_, f32[64,1,128]{2,1,0:T(1,128)} %all_to_all.16.refs_1_), custom_call_target="tpu_custom_call" | custom-call | tf_op jit(solution)/shard_map/finish/pallas_call | solution.py:258
Async XLA Ops:
  3.7 26.9 %all-to-all-start = ((f32[64,8,128]{2,1,0:T(8,128)}), f32[64,8,128]{2,1,0:T(8,128)S(1)}, u32[]{:S(2)}, u32[]{:S(2)}) async-start(f32[64,8,128]{2,1,0:T(8,128)} %bitcast.20), calls=%async_computation | async-start | bytes 524288 | tf_op jit(solution)/shard_map/all_to_all | solution.py:288
  30.6 0.7 copy-start
where the time goes:
time: 72.1 us; the launch traced here: 71.7 us
  blocking collectives  33.5 us (46%)
  starting transfers between devices  15.4 us (21%)
  Pallas kernels  12.5 us (17%)
  waiting for transfers between devices  8.98 us (12%)
    all_to_all x1, blocking collectives, trade(): lax.all_to_all(blocks, 'amp', 0, 0, tiled=True).reshape(2 * rows, LANES)  17.8 us
    all_to_all x1, blocking collectives, local(): sums = lax.all_to_all(sums, 'amp', 0, 0, tiled=True)  15.7 us
    all_to_all x1, starting transfers between devices, trade(): lax.all_to_all(blocks, 'amp', 0, 0, tiled=True).reshape(2 * rows, LANES)  15.4 us
    pallas_call x5, Pallas kernels, call(): pl.pallas_call(kernel, out_shape=shapes, in_specs=[spec(pltpu.SMEM)] * le...  12.5 us
    all_to_all x1, waiting for transfers between devices, trade(): lax.all_to_all(blocks, 'amp', 0, 0, tiled=True).reshape(2 * rows, LANES)  8.98 us
  transfers between devices with their start and end apart: 1, of which 1 were waited for; matrix products, arithmetic and copies ran while one was open for 0% of the time, Pallas kernels for 4%

commit v1 on v0

v1 whole, which is shorter than its diff:
```python
import numpy as np
import jax
import jax.numpy as jnp
from jax import lax
from jax.experimental import pallas as pl
from jax.experimental.pallas import tpu as pltpu
from jax.sharding import PartitionSpec as P

LAYERS = 2
ANGLES = 16
UNITS = 2 * (ANGLES + 1)
LANE_BITS = 7
LANES = 128

F32 = jnp.float32
BF16 = jnp.bfloat16


def angle_tables():
    steps = (np.arange(ANGLES, dtype=np.float64) + 1.0) * (np.pi / UNITS)
    return np.stack([np.cos(steps), np.sin(steps)]).astype(np.float32)


def iota(shape, dimension):
    return lax.broadcasted_iota(jnp.int32, shape, dimension)


def bit_count(values, width):
    total = values & 1
    for bit in range(1, width):
        total = total + ((values >> bit) & 1)
    return total


def split(values):
    high = values.astype(BF16)
    return high, (values - high.astype(F32)).astype(BF16)


def dot(left, right):
    return jnp.dot(left, right, preferred_element_type=F32)


def product(left, right):
    return dot(left[0], right[0]) + (dot(left[0], right[1]) + dot(left[1], right[0]))


SWAPS = 3
ROWQ, LANEQ, FREE_ROWS, SWAPPED, EARLY_ROWS, ALL_EARLY, PLAN = 0, 8, 11, 12, 13, 14, 16


def gate(bits, width):
    column = iota((1, width), 1)
    lines = []
    for place, cosine, sine in bits:
        one = ((column >> place) & 1) == 1
        lines.append((jnp.where(one, sine, cosine), jnp.where(one, cosine, -sine)))
    row = iota((8, width), 0)
    matrix = None
    for bit, (zero_line, one_line) in enumerate(lines[:3]):
        factor = jnp.where(((row >> bit) & 1) == 1, one_line, zero_line)
        matrix = factor if matrix is None else matrix * factor
    for zero_line, one_line in lines[3:]:
        matrix = jnp.concatenate([matrix * zero_line, matrix * one_line], axis=0)
    return matrix


def lane_bits(pairs):
    return [(place, cosine, -sine) for place, (cosine, sine) in enumerate(pairs)]


def pair_of(layer, rotation_ref, table_ref, qubit, keep=None):
    index = rotation_ref[layer, qubit]
    cosine, sine = table_ref[0, index], table_ref[1, index]
    if keep is None:
        return cosine, sine
    return jnp.where(keep, cosine, F32(1.0)), jnp.where(keep, sine, F32(0.0))


def cos_sin(steps):
    quarter = UNITS // 2
    turns = jnp.floor(steps * (1.0 / quarter) + 0.5)
    angle = (steps - turns * quarter) * (np.pi / UNITS)
    square = angle * angle
    sine = angle * (
        1.0 + square * (-1.0 / 6 + square * (1.0 / 120 + square * (-1.0 / 5040 + square * (1.0 / 362880))))
    )
    cosine = 1.0 + square * (
        -0.5 + square * (1.0 / 24 + square * (-1.0 / 720 + square * (1.0 / 40320)))
    )
    turns = turns.astype(jnp.int32)
    odd = (turns & 1) == 1
    cosine, sine = jnp.where(odd, sine, cosine), jnp.where(odd, cosine, sine)
    return (
        jnp.where(((turns + 1) & 2) == 2, -cosine, cosine),
        jnp.where((turns & 2) == 2, -sine, sine),
    )


def turned(cosine, sine, real, imag):
    return cosine * real + sine * imag, cosine * imag - sine * real


def parity(positions, index, bonds):
    differ = (index >> positions[:, 0:bonds]) ^ (index >> positions[:, 1 : bonds + 1])
    return (1 - 2 * (differ & 1)).astype(F32)


def fields(weights, positions, device_bits, bonds, rows):
    row_signs = parity(positions, (iota((rows, bonds), 0) << LANE_BITS) | device_bits, bonds)
    lane_signs = parity(positions, iota((LANES, bonds), 0), bonds).astype(BF16)
    stacked = jnp.concatenate([(w * row_signs).astype(BF16) for w in weights], axis=0)
    out = lax.dot_general(
        stacked, lane_signs, (((1,), (1,)), ((), ())), preferred_element_type=F32
    )
    return [out[k * rows : (k + 1) * rows] for k in range(len(weights))]


def energy(real, imag, field):
    return jnp.sum((real * real + imag * imag) * field)


def in_lanes(parts):
    lane = iota((1, LANES), 1)
    row = jnp.zeros((1, LANES), F32)
    for k, part in enumerate(parts):
        row = jnp.where(lane == k, part, row)
    return row


def evens(ref):
    half = ref.shape[0] // 2
    return ref[pl.ds(0, half, stride=2), :], ref[pl.ds(1, half, stride=2), :]


def take_blocks(ref, blocks, height, kept):
    def part(component):
        return jnp.concatenate(
            [ref[pl.ds(2 * k + component, blocks, stride=height), :] for k in range(kept)], axis=0
        )

    return part(0), part(1)


def put_blocks(ref, blocks, height, kept, real, imag):
    for k in range(kept):
        here = slice(k * blocks, (k + 1) * blocks)
        ref[pl.ds(2 * k, blocks, stride=height), :] = real[here]
        ref[pl.ds(2 * k + 1, blocks, stride=height), :] = imag[here]


def by_rows(gates, real, imag):
    both = product(gates, split(jnp.concatenate([real, imag], axis=1)))
    return both[:, :LANES], both[:, LANES:]


def by_blocks(gates, real, imag):
    size = gates[0].shape[0]
    pieces = [p[k : k + size] for p in (real, imag) for k in range(0, real.shape[0], size)]
    out = product(gates, split(jnp.concatenate(pieces, axis=1)))
    pieces = [out[:, k * LANES : (k + 1) * LANES] for k in range(len(pieces))]
    half = len(pieces) // 2
    return jnp.concatenate(pieces[:half], axis=0), jnp.concatenate(pieces[half:], axis=0)


def by_lanes(gates, real, imag):
    rows = real.shape[0]
    both = product(split(jnp.concatenate([real, imag], axis=0)), gates)
    return both[:rows], both[rows:]


def swap(buffer, plan_ref, slots):
    for i in range(SWAPS):
        @pl.when(i < plan_ref[0, SWAPPED])
        def _(i=i):
            height = 2 ** (slots - 1 - i)
            place = plan_ref[0, LANEQ + i]
            step = jnp.left_shift(jnp.int32(1), place)
            whole = buffer[...].reshape(-1, 2, height, LANES)
            low, high = whole[:, 0].reshape(-1, LANES), whole[:, 1].reshape(-1, LANES)
            one = ((iota((1, LANES), 1) >> place) & 1) == 1
            new_low = jnp.where(one, pltpu.roll(high, step, 1), low)
            new_high = jnp.where(one, high, pltpu.roll(low, LANES - step, 1))
            pairs = (new_low.reshape(-1, 1, height, LANES), new_high.reshape(-1, 1, height, LANES))
            buffer[...] = jnp.concatenate(pairs, axis=1).reshape(buffer.shape)


class Plan:
    def __init__(self, local_bits, global_bits):
        self.local_bits, self.global_bits = local_bits, global_bits
        self.qubits = local_bits + global_bits
        self.row_bits = local_bits - LANE_BITS
        self.rows = 2**self.row_bits
        self.blocks = 2**global_bits
        self.kept_bits = self.row_bits - global_bits
        self.kept = 2**self.kept_bits
        self.bonds = self.qubits - 1


def choose(plan, chain_ref, plan_ref):
    order = [chain_ref[0, k] for k in range(plan.qubits)]
    away = [(q >= plan.local_bits).astype(jnp.int32) for q in order]
    free = jnp.int32(0)
    for k, q in enumerate(order):
        near = away[k]
        if k:
            near = near | away[k - 1]
        if k + 1 < plan.qubits:
            near = near | away[k + 1]
        free = free | jnp.left_shift(1 - near, q)
    bit = lambda q: (free >> q) & 1
    row_qubits = range(LANE_BITS, plan.local_bits)
    free_rows = sum(bit(q) for q in row_qubits)
    seen = jnp.int32(0)
    for k, q in enumerate(row_qubits):
        rank = jnp.where(bit(q) == 1, seen, free_rows + k - seen)
        plan_ref[0, ROWQ + rank] = jnp.int32(q)
        seen = seen + bit(q)
    slots = plan.global_bits
    free_lanes = sum(bit(q) for q in range(LANE_BITS))
    swapped = jnp.minimum(jnp.minimum(free_lanes, SWAPS), jnp.maximum(slots - free_rows, 0))
    for i in range(SWAPS):
        plan_ref[0, LANEQ + i] = jnp.int32(-1)
    seen = jnp.int32(0)
    for q in range(LANE_BITS):
        taken = (bit(q) == 1) & (seen < swapped)
        plan_ref[0, jnp.where(taken, LANEQ + seen, PLAN - 1)] = jnp.int32(q)
        seen = seen + bit(q)
    plan_ref[0, FREE_ROWS] = free_rows
    plan_ref[0, SWAPPED] = swapped
    plan_ref[0, EARLY_ROWS] = jnp.minimum(free_rows, slots - swapped)
    plan_ref[0, ALL_EARLY] = (free_rows + swapped >= slots).astype(jnp.int32)


def touches(plan, chain, plan_ref, rows_from, rows_to, lanes):
    hit = jnp.zeros(chain.shape, jnp.int32)
    for b in range(plan.global_bits):
        wanted = (b >= rows_from) & (b < rows_to)
        hit = hit | (chain == jnp.where(wanted, plan_ref[0, ROWQ + b], -1)).astype(jnp.int32)
    if lanes:
        for i in range(SWAPS):
            hit = hit | (chain == plan_ref[0, LANEQ + i]).astype(jnp.int32)
    return (hit[:, 0 : plan.bonds] | hit[:, 1 : plan.bonds + 1]).astype(F32)


def ordered_positions(plan, chain, plan_ref):
    places = chain
    for b in range(plan.row_bits):
        places = jnp.where(chain == plan_ref[0, ROWQ + b], LANE_BITS + b, places)
    return places


def moved_positions(plan, chain, plan_ref):
    slots, swapped = plan.global_bits, plan_ref[0, SWAPPED]
    places = jnp.where(chain >= plan.local_bits, chain - plan.local_bits + LANE_BITS, chain)
    for b in range(plan.row_bits):
        target = jnp.int32(LANE_BITS + b)
        if b < slots:
            target = jnp.int32(plan.local_bits + b)
            i = slots - 1 - b
            if i < SWAPS:
                target = jnp.where(i < swapped, plan_ref[0, LANEQ + i], target)
        places = jnp.where(chain == plan_ref[0, ROWQ + b], target, places)
    for i in range(SWAPS):
        places = jnp.where(chain == plan_ref[0, LANEQ + i], plan.local_bits + slots - 1 - i, places)
    return places


def row_ones(plan, device):
    ones = bit_count(iota((plan.rows, LANES), 0), plan.row_bits)
    return ones + bit_count(iota((plan.rows, LANES), 1), LANE_BITS) + bit_count(device, plan.global_bits)


def first_kernel(
    plan, rotation_ref, table_ref, order_ref, chain_ref, coupling_ref, bond_ref, amps_ref,
    out_ref, sums_ref, plan_ref, buffer,
):
    device = lax.axis_index("amp")
    bonds, rows = plan.bonds, plan.rows
    choose(plan, order_ref, plan_ref)
    chain = chain_ref[...]
    device_bits = device << plan.local_bits
    bond_signs = (2 * bond_ref[...] - 1).astype(F32)
    (steps,) = fields(
        [(coupling_ref[0:1, :] + 1).astype(F32) * bond_signs], chain, device_bits, bonds, rows
    )
    steps = steps + (UNITS // 2) * row_ones(plan, device).astype(F32)
    pair = lambda layer, q, keep=None: pair_of(layer, rotation_ref, table_ref, q, keep)

    real, imag = evens(amps_ref)
    norm = jnp.sum(real * real + imag * imag)
    real, imag = turned(*cos_sin(steps), real, imag)
    ranked = [plan_ref[0, ROWQ + b] for b in range(plan.row_bits)]
    row_gate = gate([(q - LANE_BITS, *pair(0, q)) for q in ranked], rows)
    lane_gate = gate(lane_bits([pair(0, q) for q in range(LANE_BITS)]), LANES)
    real, imag = by_rows(split(row_gate), real, imag)
    real, imag = by_lanes(split(lane_gate), real, imag)

    early = touches(plan, chain, plan_ref, 0, plan_ref[0, EARLY_ROWS], True)
    weight = early * bond_signs
    steps, signs = fields(
        [(coupling_ref[1:2, :] + 1).astype(F32) * weight, weight],
        ordered_positions(plan, chain, plan_ref), device_bits, bonds, rows,
    )
    sums_ref[...] = in_lanes([norm, energy(real, imag, signs)])
    real, imag = turned(*cos_sin(steps), real, imag)
    bits = []
    for b in range(plan.global_bits):
        bits.append((b, *pair(1, ranked[b], b < plan_ref[0, EARLY_ROWS])))
    real, imag = by_blocks(split(gate(bits, plan.blocks)), real, imag)
    pairs = []
    for q in range(LANE_BITS):
        keep = q == plan_ref[0, LANEQ]
        for i in range(1, SWAPS):
            keep = keep | (q == plan_ref[0, LANEQ + i])
        pairs.append(pair(1, q, keep))
    real, imag = by_lanes(split(gate(lane_bits(pairs), LANES)), real, imag)
    buffer[...] = jnp.concatenate([real, imag], axis=0)
    swap(buffer, plan_ref, plan.global_bits)
    put_blocks(out_ref, plan.blocks, 2 * plan.kept, plan.kept, buffer[:rows], buffer[rows:])


def prepare_kernel(
    plan, rotation_ref, table_ref, plan_ref, chain_ref, coupling_ref, bond_ref,
    cosine_ref, sine_ref, before_ref, after_ref, late_ref, *gate_refs,
):
    device = lax.axis_index("amp")
    bonds, rows, slots = plan.bonds, plan.rows, plan.global_bits
    chain = chain_ref[...]
    bond_signs = (2 * bond_ref[...] - 1).astype(F32)
    early_rows, swapped = plan_ref[0, EARLY_ROWS], plan_ref[0, SWAPPED]
    rest = bond_signs * (1.0 - touches(plan, chain, plan_ref, 0, early_rows, True))
    late = bond_signs * touches(plan, chain, plan_ref, early_rows, slots - swapped, False)
    steps, before_ref[...], after_ref[...] = fields(
        [(coupling_ref[1:2, :] + 1).astype(F32) * rest, rest, bond_signs - late],
        moved_positions(plan, chain, plan_ref), device << plan.local_bits, bonds, rows,
    )
    cosine_ref[...], sine_ref[...] = cos_sin(steps)
    (late_ref[...],) = fields([late], chain, device << plan.local_bits, bonds, rows)
    pair = lambda layer, q, keep=None: pair_of(layer, rotation_ref, table_ref, q, keep)
    ranked = [plan_ref[0, ROWQ + b] for b in range(plan.row_bits)]
    far = [plan.local_bits + b for b in range(slots)]
    lane_pairs = []
    for q in range(LANE_BITS):
        held = jnp.int32(q)
        for i in range(SWAPS):
            held = jnp.where(plan_ref[0, LANEQ + i] == q, ranked[slots - 1 - i], held)
        lane_pairs.append(pair(1, held))
    back = []
    for b in range(plan.row_bits):
        wanted = (b >= early_rows) & (b < slots - swapped)
        cosine, sine = pair(1, ranked[b], wanted)
        back.append((ranked[b] - LANE_BITS, cosine, -sine))
    gates = [
        gate([(b, *pair(0, q)) for b, q in enumerate(far)], plan.blocks),
        gate([(b, *pair(1, q)) for b, q in enumerate(far + ranked[slots:])], rows),
        gate(lane_bits(lane_pairs), LANES),
        gate(back, rows).T,
    ]
    for k, made in enumerate(gates):
        gate_refs[2 * k][...], gate_refs[2 * k + 1][...] = split(made)


def middle_kernel(plan, state_ref, cosine_ref, sine_ref, before_ref, after_ref, sums_ref, *refs):
    (ga, gb, ha, hb, la, lb), (out_ref,) = refs[:6], refs[6:]
    blocks, kept = plan.blocks, plan.kept
    real, imag = take_blocks(state_ref, blocks, 2 * kept, kept)
    real, imag = by_blocks((ga[...], gb[...]), real, imag)
    before = energy(real, imag, before_ref[...])
    real, imag = turned(cosine_ref[...], sine_ref[...], real, imag)
    real, imag = by_rows((ha[...], hb[...]), real, imag)
    real, imag = by_lanes((la[...], lb[...]), real, imag)
    after = energy(real, imag, after_ref[...])
    height = 2 * kept + 1
    put_blocks(out_ref, blocks, height, kept, real, imag)
    sums = sums_ref[...] + in_lanes([F32(0.0), before, after])
    out_ref[pl.ds(2 * kept, blocks, stride=height), :] = jnp.broadcast_to(sums, (blocks, LANES))


def last_kernel(plan, plan_ref, state_ref, late_ref, ga, gb, out_ref, energies_ref, late_out_ref, buffer):
    device = lax.axis_index("amp")
    blocks, kept, rows = plan.blocks, plan.kept, plan.rows
    height = 2 * kept + 1
    sums = jnp.sum(state_ref[pl.ds(2 * kept, blocks, stride=height), :], axis=0, keepdims=True)
    amps = float(2**plan.qubits)
    mean = sums[:, 0:1] / amps + 1e-06
    factor = 1.0 / jnp.sqrt(mean)
    square = factor * factor / amps
    energies_ref[...] = sums[:, 1 : 1 + LAYERS] * square
    real, imag = take_blocks(state_ref, blocks, height, kept)
    buffer[...] = jnp.concatenate([real, imag], axis=0)
    swap(buffer, plan_ref, plan.global_bits)
    real, imag = by_rows((ga[...], gb[...]), buffer[:rows], buffer[rows:])
    late_out_ref[...] = in_lanes([0.0, energy(real, imag, late_ref[...])])[:, 0:LAYERS] * square
    ones = row_ones(plan, device)
    odd = (ones & 1) == 1
    real, imag = jnp.where(odd, imag, real), jnp.where(odd, real, imag)
    real = jnp.where(((ones + 1) & 2) == 2, -factor, factor) * real
    imag = jnp.where((ones & 2) == 2, -factor, factor) * imag
    out_ref[pl.ds(0, rows, stride=2), :] = real
    out_ref[pl.ds(1, rows, stride=2), :] = imag


def spec(space):
    return pl.BlockSpec(memory_space=space)


def call(kernel, shapes, scalars, arrays, name, spaces=None, scratch=()):
    return pl.pallas_call(
        kernel,
        out_shape=shapes,
        in_specs=[spec(pltpu.SMEM)] * len(scalars) + [spec(pltpu.VMEM)] * len(arrays),
        out_specs=tuple(spec(s) for s in spaces or (pltpu.VMEM,) * len(shapes)),
        scratch_shapes=scratch,
        name=name,
    )(*scalars, *arrays)


def local(amplitudes, coupling_index, rotation_index, chain_order, bond_sign):
    local_bits = amplitudes.shape[1].bit_length() - 1
    size = lax.axis_size("amp")
    plan = Plan(local_bits, size.bit_length() - 1)
    rows = plan.rows
    shape = jax.ShapeDtypeStruct
    bind = lambda kernel: lambda *refs: kernel(plan, *refs)

    state = amplitudes.reshape(2, rows, LANES).transpose(1, 0, 2).reshape(2 * rows, LANES)
    table = jnp.asarray(angle_tables())
    chain, bond = chain_order.reshape(1, -1), bond_sign.reshape(1, -1)
    small = (chain, coupling_index, bond)
    whole = shape((2 * rows, LANES), F32)
    field = shape((rows, LANES), F32)
    square_of = lambda n: shape((n, n), BF16)
    buffer = (pltpu.VMEM((2 * rows, LANES), F32),)

    state, sums, chosen = call(
        bind(first_kernel),
        (whole, shape((1, LANES), F32), shape((1, PLAN), jnp.int32)),
        (rotation_index, table, chain), (*small, state), "first",
        (pltpu.VMEM, pltpu.VMEM, pltpu.SMEM), buffer,
    )
    sizes = (size, rows, LANES, rows)
    made = call(
        bind(prepare_kernel), (field,) * 5 + tuple(square_of(n) for n in sizes for _ in range(2)),
        (rotation_index, table, chosen), small, "prepare",
    )
    fields_made, late, gates = made[:4], made[4], made[5:]
    state = lax.all_to_all(state.reshape(size, 2 * plan.kept, LANES), "amp", 0, 0, tiled=True)
    height = 2 * plan.kept + 1
    (state,) = call(
        bind(middle_kernel), (shape((size * height, LANES), F32),), (),
        (state.reshape(2 * rows, LANES), *fields_made, sums, *gates[:6]), "middle",
    )
    state = lax.all_to_all(state.reshape(size, height, 1, LANES), "amp", 0, 0, tiled=True)
    pair = shape((1, LAYERS), F32)
    state, energies, extra = call(
        bind(last_kernel), (whole, pair, pair), (chosen,),
        (state.reshape(size * height, LANES), late, *gates[6:]), "last", scratch=buffer,
    )

    def with_late(energies, extra):
        sent = jnp.broadcast_to(extra[None], (size, 1, LAYERS))
        return energies + lax.all_to_all(sent, "amp", 0, 0, tiled=True).sum(axis=0)

    energies = lax.cond(
        chosen[0, ALL_EARLY] == 1, lambda energies, extra: energies, with_late, energies, extra
    )
    final = state.reshape(rows, 2, LANES).transpose(1, 0, 2).reshape(2, rows * LANES)
    return final, energies.reshape(LAYERS)


def solution(mesh):
    in_specs = (P(None, ("rep", "amp")), P("rep", None), P("rep", None), P(), P())
    out_specs = (P(None, ("rep", "amp")), P("rep"))
    return jax.shard_map(local, mesh=mesh, in_specs=in_specs, out_specs=out_specs, check_vma=False)
```

time: 72.1 us -> 57.7 us (0.80)
  blocking collectives: 33.5 us -> 0 us
  waiting for transfers between devices: 8.98 us -> 20 us
  starting transfers between devices: 15.4 us -> 21.6 us
  local copies, waits for them, and re-layouts: 0.7 us -> 2.52 us
  Pallas kernels: 12.5 us -> 11.7 us
    all_to_all x2 -> x0, blocking collectives: 33.5 us -> none  [the longest x1 17.8 us: trade(): lax.all_to_all(blocks, 'amp', 0, 0, tiled=True).reshape(2 * rows, LANES)]
    all_to_all x1 -> x2, waiting for transfers between devices: 8.98 us -> 20 us  [the longest x1 10.8 us: local(): lax.all_to_all(state.reshape(size, height, 1, LANES), 'amp', 0, 0, tiled=...]
    all_to_all x1 -> x2, starting transfers between devices: 15.4 us -> 21.6 us  [the longest x1 15.4 us: local(): lax.all_to_all(state.reshape(size, 2 * plan.kept, LANES), 'amp', 0, 0, ti...]
    unnamed x2 -> x9, local copies, waits for them, and re-layouts: 0.7 us -> 1.94 us
    pallas_call x5 -> x4, Pallas kernels: 12.5 us -> 11.7 us  [call(): pl.pallas_call(kernel, out_shape=shapes, in_specs=[spec(pltpu.SMEM)] * le...]
  transfers between devices with their start and end apart: 1 -> 2, of which waited for: 1 -> 2; matrix products, arithmetic and copies ran while one was open for 0% -> 1% of each run, Pallas kernels for 4% -> 4%
where the time goes in v1:
time: 57.7 us; the launch traced here: 57.2 us
  starting transfers between devices  21.6 us (37%)
  waiting for transfers between devices  20 us (35%)
  Pallas kernels  11.7 us (20%)
  local copies, waits for them, and re-layouts  2.52 us (4%)
  between operations  1.32 us (2%)
    all_to_all x1, starting transfers between devices, local(): lax.all_to_all(state.reshape(size, 2 * plan.kept, LANES), 'amp', 0, 0, ti...  15.4 us
    pallas_call x4, Pallas kernels, call(): pl.pallas_call(kernel, out_shape=shapes, in_specs=[spec(pltpu.SMEM)] * le...  11.7 us
    all_to_all x1, waiting for transfers between devices, local(): lax.all_to_all(state.reshape(size, height, 1, LANES), 'amp', 0, 0, tiled=...  10.8 us
    all_to_all x1, waiting for transfers between devices, local(): lax.all_to_all(state.reshape(size, 2 * plan.kept, LANES), 'amp', 0, 0, ti...  9.19 us
    all_to_all x1, starting transfers between devices, local(): lax.all_to_all(state.reshape(size, height, 1, LANES), 'amp', 0, 0, tiled=...  6.2 us
    unnamed x9, local copies, waits for them, and re-layouts  1.94 us
  transfers between devices with their start and end apart: 2, of which 2 were waited for; matrix products, arithmetic and copies ran while one was open for 1% of the time, Pallas kernels for 4%

profile of v1, /device:TPU:1, one launch (start us, length us, event | category | flops | bytes accessed | tf_op | source)
XLA Modules:
  0.0 57.2 jit_solution(16281011720392806162)
XLA Ops:
  0.6 3.7 %first.1 = (f32[512,128]{1,0:T(8,128)}, f32[1,128]{1,0:T(1,128)}, s32[1,16]{1,0:T(1,128)}) custom-call(s32[2,21]{1,0:T(2,128)} %refs_0_.3, f32[2,16]{1,0:T(2,128)} %constant.7.clone.refs_1_, s32[1,21]{1,0:T(1,128)} %bitcast.30, s32[1,21]{1,0:T(1,128)} %bitcast.31, s32[2,20]{1,0:T(2,128)} %refs_4_.3, s32[1,20]{1,0:T(1,128)} %bitcast.33, f32[512,128]{1,0:T(8,128)} %bitcast.28), custom_call_target="tpu_custom_call" | custom-call | tf_op jit(solution)/shard_map/first/pallas_call | solution.py:409
  4.3 15.4 %all-to-all-start.1 = ((f32[64,8,128]{2,1,0:T(8,128)}), f32[64,8,128]{2,1,0:T(8,128)S(1)}, u32[]{:S(2)}, u32[]{:S(2)}) async-start(f32[64,8,128]{2,1,0:T(8,128)} %bitcast.29), calls=%async_computation.1 | async-start | bytes 524288 | tf_op jit(solution)/shard_map/all_to_all | solution.py:448
  19.7 2.3 %prepare.1 = (f32[256,128]{1,0:T(8,128)}, f32[256,128]{1,0:T(8,128)}, f32[256,128]{1,0:T(8,128)}, f32[256,128]{1,0:T(8,128)}, f32[256,128]{1,0:T(8,128)}, /*inde...) custom-call(s32[2,21]{1,0:T(2,128)} %refs_0_.3, ...), custom_call_target="tpu_custom_call" | custom-call | tf_op jit(solution)/shard_map/prepare/pallas_call | solution.py:409
  22.1 9.2 %all-to-all-done.1 = f32[64,8,128]{2,1,0:T(8,128)S(1)} async-done(((f32[64,8,128]{2,1,0:T(8,128)}), f32[64,8,128]{2,1,0:T(8,128)S(1)}, u32[]{:S(2)}, u32[]{:S(2)}) %all-to-all-start.1) | async-done | bytes 262176 | tf_op jit(solution)/shard_map/all_to_all | solution.py:448
  31.3 0.0 copy-start.1
  31.3 0.7 %copy-done.1 = f32[64,8,128]{2,1,0:T(8,128)} copy-done((f32[64,8,128]{2,1,0:T(8,128)}, f32[64,8,128]{2,1,0:T(8,128)S(1)}, u32[]{:S(2)}) %copy-start.1) | copy-done | bytes 262168
  32.0 3.1 %middle.1 = f32[576,128]{1,0:T(8,128)} custom-call(f32[512,128]{1,0:T(8,128)} %bitcast.27, f32[256,128]{1,0:T(8,128)} %get-tuple-element.35.refs_1_, f32[256,128]{1,0:T(8,128)} %get-tuple-element.36.refs_2_, f32[256,128]{1,0:T(8,128)} %get-tuple-element.37.refs_3_, f32[256,128]{1,0:T(8,128)} %get-tuple-element.38.refs_4_, ...), custom_call_target="tpu_custom_call" | custom-call | tf_op jit(solution)/shard_map/middle/pallas_call | solution.py:409
  35.0 0.0 copy-start.2
  35.0 6.2 %all-to-all-start.2 = ((f32[64,9,1,128]{3,2,1,0:T(1,128)}), f32[64,9,1,128]{3,2,1,0:T(1,128)S(1)}, u32[]{:S(2)}, u32[]{:S(2)}) async-start(f32[64,9,1,128]{3,2,1,0:T(1,128)} %bitcast.26), calls=%async_computation.2 | async-start | bytes 589824 | tf_op jit(solution)/shard_map/all_to_all | solution.py:454
  41.3 0.0 copy-done.2
  41.3 0.6 %slice.3 = s32[1,1]{1,0:T(1,128)} slice(s32[1,16]{1,0:T(1,128)S(1)} %copy-done.2), slice={[0:1], [14:15]} | slice | bytes 8 | tf_op jit(solution)/shard_map/slice | solution.py:466
  42.5 10.8 %all-to-all-done.2 = f32[64,9,1,128]{3,2,1,0:T(1,128)S(1)} async-done(((f32[64,9,1,128]{3,2,1,0:T(1,128)}), f32[64,9,1,128]{3,2,1,0:T(1,128)S(1)}, u32[]{:S(2)}, u32[]{:S(2)}) %all-to-all-start.2) | async-done | bytes 294944 | tf_op jit(solution)/shard_map/all_to_all | solution.py:454
  53.3 0.0 copy-start
  53.3 0.7 %copy-done = f32[64,9,1,128]{3,2,1,0:T(1,128)} copy-done((f32[64,9,1,128]{3,2,1,0:T(1,128)}, f32[64,9,1,128]{3,2,1,0:T(1,128)S(1)}, u32[]{:S(2)}) %copy-start) | copy-done | bytes 294936
  54.1 2.6 %last.1 = (f32[512,128]{1,0:T(8,128)}, f32[1,2]{1,0:T(1,128)S(1)}, f32[1,2]{1,0:T(1,128)S(1)}) custom-call(s32[1,16]{1,0:T(1,128)} %get-tuple-element.33.refs_2_.refs_0_, f32[576,128]{1,0:T(8,128)} %bitcast.25, f32[256,128]{1,0:T(8,128)} %get-tuple-element.46.refs_2_, bf16[256,256]{1,0:T(8,128)(2,1)} %get-tuple-element.47.refs_3_, ...), custom_call_target="tpu_custom_call" | custom-call | tf_op jit(solution)/shard_map/last/pallas_call | solution.py:409
  56.7 0.0 copy-start.3
  56.7 0.5 copy-done.3
  (2 shorter events, 0.0 us)
Async XLA Ops:
  4.3 26.9 %all-to-all-start.1 = ((f32[64,8,128]{2,1,0:T(8,128)}), f32[64,8,128]{2,1,0:T(8,128)S(1)}, u32[]{:S(2)}, u32[]{:S(2)}) async-start(f32[64,8,128]{2,1,0:T(8,128)} %bitcast.29), calls=%async_computation.1 | async-start | bytes 524288 | tf_op jit(solution)/shard_map/all_to_all | solution.py:448
  31.3 0.7 %copy-start.1 = (f32[64,8,128]{2,1,0:T(8,128)}, f32[64,8,128]{2,1,0:T(8,128)S(1)}, u32[]{:S(2)}) copy-start(f32[64,8,128]{2,1,0:T(8,128)S(1)} %all-to-all-done.1) | copy-start | bytes 786436
  35.0 6.2 %copy-start.2 = (s32[1,16]{1,0:T(1,128)S(1)}, s32[1,16]{1,0:T(1,128)}, u32[]{:S(2)}) copy-start(s32[1,16]{1,0:T(1,128)} %get-tuple-element.33.refs_2_.refs_0_) | copy-start | bytes 196
  35.0 18.3 %all-to-all-start.2 = ((f32[64,9,1,128]{3,2,1,0:T(1,128)}), f32[64,9,1,128]{3,2,1,0:T(1,128)S(1)}, u32[]{:S(2)}, u32[]{:S(2)}) async-start(f32[64,9,1,128]{3,2,1,0:T(1,128)} %bitcast.26), calls=%async_computation.2 | async-start | bytes 589824 | tf_op jit(solution)/shard_map/all_to_all | solution.py:454
  53.3 0.7 %copy-start = (f32[64,9,1,128]{3,2,1,0:T(1,128)}, f32[64,9,1,128]{3,2,1,0:T(1,128)S(1)}, u32[]{:S(2)}) copy-start(f32[64,9,1,128]{3,2,1,0:T(1,128)S(1)} %all-to-all-done.2) | copy-start | bytes 884740
  56.7 0.5 copy-start.3

commit v2 on v1

--- a/solution.py
+++ b/solution.py
@@ -322,8 +322,9 @@
 
 def prepare_kernel(
     plan, rotation_ref, table_ref, plan_ref, chain_ref, coupling_ref, bond_ref,
-    cosine_ref, sine_ref, before_ref, after_ref, late_ref, *gate_refs,
+    done_ref, cosine_ref, sine_ref, before_ref, after_ref, late_ref, *gate_refs,
 ):
+    done_ref[0, 0] = plan_ref[0, ALL_EARLY]
     device = lax.axis_index("amp")
     bonds, rows, slots = plan.bonds, plan.rows, plan.global_bits
     chain = chain_ref[...]
@@ -377,7 +378,8 @@
     out_ref[pl.ds(2 * kept, blocks, stride=height), :] = jnp.broadcast_to(sums, (blocks, LANES))
 
 
-def last_kernel(plan, plan_ref, state_ref, late_ref, ga, gb, out_ref, energies_ref, late_out_ref, buffer):
+def last_kernel(plan, plan_ref, state_ref, ga, gb, *refs):
+    late_ref, (out_ref, energies_ref, *late_out_ref, buffer) = refs[:-3][:1], refs[-4 if len(refs) == 5 else -3 :]
     device = lax.axis_index("amp")
     blocks, kept, rows = plan.blocks, plan.kept, plan.rows
     height = 2 * kept + 1
@@ -391,7 +393,8 @@
     buffer[...] = jnp.concatenate([real, imag], axis=0)
     swap(buffer, plan_ref, plan.global_bits)
     real, imag = by_rows((ga[...], gb[...]), buffer[:rows], buffer[rows:])
-    late_out_ref[...] = in_lanes([0.0, energy(real, imag, late_ref[...])])[:, 0:LAYERS] * square
+    if late_ref:
+        late_out_ref[0][...] = in_lanes([0.0, energy(real, imag, late_ref[0][...])])[:, 0:LAYERS] * square
     ones = row_ones(plan, device)
     odd = (ones & 1) == 1
     real, imag = jnp.where(odd, imag, real), jnp.where(odd, real, imag)
@@ -405,7 +408,13 @@
     return pl.BlockSpec(memory_space=space)
 
 
-def call(kernel, shapes, scalars, arrays, name, spaces=None, scratch=()):
+def call(kernel, shapes, scalars, arrays, name, spaces=None, scratch=(), near=0, held=()):
+    kept = len(arrays) - near
+    arrays = tuple(
+        pltpu.with_memory_space_constraint(a, pltpu.VMEM) if k >= kept else a
+        for k, a in enumerate(arrays)
+    )
+    shapes = tuple(pltpu.VMEM(s.shape, s.dtype) if k in held else s for k, s in enumerate(shapes))
     return pl.pallas_call(
         kernel,
         out_shape=shapes,
@@ -437,36 +446,48 @@
         bind(first_kernel),
         (whole, shape((1, LANES), F32), shape((1, PLAN), jnp.int32)),
         (rotation_index, table, chain), (*small, state), "first",
-        (pltpu.VMEM, pltpu.VMEM, pltpu.SMEM), buffer,
+        (pltpu.VMEM, pltpu.VMEM, pltpu.SMEM), buffer, held=(0, 1),
     )
     sizes = (size, rows, LANES, rows)
     made = call(
-        bind(prepare_kernel), (field,) * 5 + tuple(square_of(n) for n in sizes for _ in range(2)),
+        bind(prepare_kernel),
+        (shape((1, 1), jnp.int32),) + (field,) * 5 + tuple(square_of(n) for n in sizes for _ in range(2)),
         (rotation_index, table, chosen), small, "prepare",
-    )
-    fields_made, late, gates = made[:4], made[4], made[5:]
+        (pltpu.SMEM,) + (pltpu.VMEM,) * 13, held=range(1, 14),
+    )
+    done, fields_made, late, gates = made[0], made[1:5], made[5], made[6:]
     state = lax.all_to_all(state.reshape(size, 2 * plan.kept, LANES), "amp", 0, 0, tiled=True)
     height = 2 * plan.kept + 1
     (state,) = call(
         bind(middle_kernel), (shape((size * height, LANES), F32),), (),
-        (state.reshape(2 * rows, LANES), *fields_made, sums, *gates[:6]), "middle",
+        (state.reshape(2 * rows, LANES), *fields_made, sums, *gates[:6]), "middle", near=12, held=(0,),
     )
     state = lax.all_to_all(state.reshape(size, height, 1, LANES), "amp", 0, 0, tiled=True)
     pair = shape((1, LAYERS), F32)
-    state, energies, extra = call(
-        bind(last_kernel), (whole, pair, pair), (chosen,),
-        (state.reshape(size * height, LANES), late, *gates[6:]), "last", scratch=buffer,
-    )
-
-    def with_late(energies, extra):
+
+    def end(chosen, state, ga, gb, *late):
+        return call(
+            bind(last_kernel), (whole, pair) + (pair,) * len(late), (chosen,),
+            (state, ga, gb, *late), "last", scratch=buffer, near=3 + len(late),
+        )
+
+    def apart(final):
+        return final.reshape(rows, 2, LANES).transpose(1, 0, 2).reshape(2, rows * LANES)
+
+    def early_end(*operands):
+        final, energies = end(*operands[:-1])
+        return apart(final), energies.reshape(LAYERS)
+
+    def late_end(*operands):
+        final, energies, extra = end(*operands)
         sent = jnp.broadcast_to(extra[None], (size, 1, LAYERS))
-        return energies + lax.all_to_all(sent, "amp", 0, 0, tiled=True).sum(axis=0)
-
-    energies = lax.cond(
-        chosen[0, ALL_EARLY] == 1, lambda energies, extra: energies, with_late, energies, extra
-    )
-    final = state.reshape(rows, 2, LANES).transpose(1, 0, 2).reshape(2, rows * LANES)
-    return final, energies.reshape(LAYERS)
+        total = energies + lax.all_to_all(sent, "amp", 0, 0, tiled=True).sum(axis=0)
+        return apart(final), total.reshape(LAYERS)
+
+    return lax.cond(
+        done[0, 0] == 1, early_end, late_end,
+        chosen, state.reshape(size * height, LANES), *gates[6:], late,
+    )
 
 
 def solution(mesh):

time: 57.7 us -> 53.6 us (0.929)
  local copies, waits for them, and re-layouts: 2.52 us -> 0 us
  Pallas kernels: 11.7 us -> 9.29 us
  waiting for transfers between devices: 20 us -> 21.2 us
    pallas_call x4, Pallas kernels: 11.7 us -> 9.29 us  [call(): pl.pallas_call(kernel, out_shape=shapes, in_specs=[spec(pltpu.SMEM)] * le...]
    unnamed x9 -> x0, local copies, waits for them, and re-layouts: 1.94 us -> none
    all_to_all x1, waiting for transfers between devices: 9.19 us -> 9.79 us  [local(): lax.all_to_all(state.reshape(size, 2 * plan.kept, LANES), 'amp', 0, 0, ti...]
    all_to_all x1, waiting for transfers between devices: 10.8 us -> 11.4 us  [local(): lax.all_to_all(state.reshape(size, height, 1, LANES), 'amp', 0, 0, tiled=...]
    slice x1 -> x0, local copies, waits for them, and re-layouts: 0.58 us -> none  [local(): chosen[0, ALL_EARLY] == 1]
  transfers between devices with their start and end apart: 2 -> 2, of which waited for: 2 -> 2; matrix products, arithmetic and copies ran while one was open for 1% -> 0% of each run, Pallas kernels for 4% -> 3%
where the time goes in v2:
time: 53.6 us; the launch traced here: 53.3 us
  starting transfers between devices  21.5 us (40%)
  waiting for transfers between devices  21.2 us (40%)
  Pallas kernels  9.29 us (17%)
  between operations  1.31 us (2%)
    all_to_all x1, starting transfers between devices, local(): lax.all_to_all(state.reshape(size, 2 * plan.kept, LANES), 'amp', 0, 0, ti...  15.4 us
    all_to_all x1, waiting for transfers between devices, local(): lax.all_to_all(state.reshape(size, height, 1, LANES), 'amp', 0, 0, tiled=...  11.4 us
    all_to_all x1, waiting for transfers between devices, local(): lax.all_to_all(state.reshape(size, 2 * plan.kept, LANES), 'amp', 0, 0, ti...  9.79 us
    pallas_call x4, Pallas kernels, call(): pl.pallas_call(kernel, out_shape=shapes, in_specs=[spec(pltpu.SMEM)] * le...  9.29 us
    all_to_all x1, starting transfers between devices, local(): lax.all_to_all(state.reshape(size, height, 1, LANES), 'amp', 0, 0, tiled=...  6.07 us
  transfers between devices with their start and end apart: 2, of which 2 were waited for; matrix products, arithmetic and copies ran while one was open for 0% of the time, Pallas kernels for 3%

profile of v2, /device:TPU:1, one launch (start us, length us, event | category | flops | bytes accessed | tf_op | source)
XLA Modules:
  0.0 53.3 jit_solution(18030205082048751112)
XLA Ops:
  0.6 3.8 %first.1 = (f32[512,128]{1,0:T(8,128)}, f32[1,128]{1,0:T(1,128)S(1)}, s32[1,16]{1,0:T(1,128)S(1)}) custom-call(s32[2,21]{1,0:T(2,128)} %refs_0_.3, f32[2,16]{1,0:T(2,128)} %constant.7.clone.refs_1_, s32[1,21]{1,0:T(1,128)} %bitcast.34, s32[1,21]{1,0:T(1,128)} %bitcast.35, s32[2,20]{1,0:T(2,128)} %refs_4_.3, s32[1,20]{1,0:T(1,128)} %bitcast.37, ...), custom_call_target="tpu_custom_call" | custom-call | tf_op jit(solution)/shard_map/first/pallas_call | solution.py:418
  4.5 15.4 %all-to-all-start.1 = ((f32[64,8,128]{2,1,0:T(8,128)}), f32[64,8,128]{2,1,0:T(8,128)S(1)}, u32[]{:S(2)}, u32[]{:S(2)}) async-start(f32[64,8,128]{2,1,0:T(8,128)} %bitcast.20), calls=%async_computation.1 | async-start | bytes 524288 | tf_op jit(solution)/shard_map/all_to_all | solution.py:459
  19.9 1.7 %prepare.1 = (s32[1,1]{1,0:T(1,128)}, f32[256,128]{1,0:T(8,128)S(1)}, f32[256,128]{1,0:T(8,128)S(1)}, f32[256,128]{1,0:T(8,128)S(1)}, f32[256,128]{1,0:T(8,128)S...) custom-call(s32[2,21]{1,0:T(2,128)} %refs_0_.3, ...), custom_call_target="tpu_custom_call" | custom-call | tf_op jit(solution)/shard_map/prepare/pallas_call | solution.py:418
  21.6 9.8 %all-to-all-done.1 = f32[64,8,128]{2,1,0:T(8,128)S(1)} async-done(((f32[64,8,128]{2,1,0:T(8,128)}), f32[64,8,128]{2,1,0:T(8,128)S(1)}, u32[]{:S(2)}, u32[]{:S(2)}) %all-to-all-start.1) | async-done | bytes 262176 | tf_op jit(solution)/shard_map/all_to_all | solution.py:459
  31.4 1.8 %middle.1 = f32[576,128]{1,0:T(8,128)} custom-call(f32[512,128]{1,0:T(8,128)S(1)} %bitcast.32, f32[256,128]{1,0:T(8,128)S(1)} %get-tuple-element.54.refs_1_, f32[256,128]{1,0:T(8,128)S(1)} %get-tuple-element.55.refs_2_, f32[256,128]{1,0:T(8,128)S(1)} %get-tuple-element.56.refs_3_, f32[256,128]{1,0:T(8,128)S(1)} %get-tuple-element.57.refs_4_, ...), custom_call_target="tpu_custom_call" | custom-call | tf_op jit(solution)/shard_map/middle/pallas_call | solution.py:418
  33.2 6.1 %all-to-all-start.2 = ((f32[64,9,1,128]{3,2,1,0:T(1,128)}), f32[64,9,1,128]{3,2,1,0:T(1,128)S(1)}, u32[]{:S(2)}, u32[]{:S(2)}) async-start(f32[64,9,1,128]{3,2,1,0:T(1,128)} %bitcast.22), calls=%async_computation.2 | async-start | bytes 589824 | tf_op jit(solution)/shard_map/all_to_all | solution.py:465
  39.9 11.4 %all-to-all-done.2 = f32[64,9,1,128]{3,2,1,0:T(1,128)S(1)} async-done(((f32[64,9,1,128]{3,2,1,0:T(1,128)}), f32[64,9,1,128]{3,2,1,0:T(1,128)S(1)}, u32[]{:S(2)}, u32[]{:S(2)}) %all-to-all-start.2) | async-done | bytes 294944 | tf_op jit(solution)/shard_map/all_to_all | solution.py:465
  51.3 2.0 %conditional.1 = (f32[2,32768]{1,0:T(2,128)}, f32[2]{0:T(128)}) conditional(s32[]{:T(128)} %bitcast.19, (s32[1,16]{1,0:T(1,128)S(1)}, f32[576,128]{1,0:T(8,128)S(1)}, bf16[256,256]{1,0:T(8,128)(2,1)S(1)}, bf16[256,256]{1,0:T(8,128)(2,1)S(1)}, f32[256,128]{1,0:T(8,128)S(1)}) %tuple.23, (s32[1,16]{1,0:T(1,128)S(1)}, f32[576,128]{1,0:T(8,128)S(1)}, ...), branch_computations={%region_0.0_spmd, %region_2.0_spmd} | conditional | flops 128 | bytes 2228 | solution.py:487
  51.3 2.0 %last.3 = (f32[512,128]{1,0:T(8,128)}, f32[1,2]{1,0:T(1,128)}) custom-call(s32[1,16]{1,0:T(1,128)S(1)} %get-tuple-element.26.refs_0_, f32[576,128]{1,0:T(8,128)S(1)} %get-tuple-element.27.refs_1_, bf16[256,256]{1,0:T(8,128)(2,1)S(1)} %get-tuple-element.28.refs_2_, bf16[256,256]{1,0:T(8,128)(2,1)S(1)} %get-tuple-element.29.refs_3_), custom_call_target="tpu_custom_call" | custom-call | tf_op jit(solution)/shard_map/cond/branch_1_fun/last/pallas_call | solution.py:418
Async XLA Ops:
  4.5 26.9 %all-to-all-start.1 = ((f32[64,8,128]{2,1,0:T(8,128)}), f32[64,8,128]{2,1,0:T(8,128)S(1)}, u32[]{:S(2)}, u32[]{:S(2)}) async-start(f32[64,8,128]{2,1,0:T(8,128)} %bitcast.20), calls=%async_computation.1 | async-start | bytes 524288 | tf_op jit(solution)/shard_map/all_to_all | solution.py:459
  33.2 18.2 %all-to-all-start.2 = ((f32[64,9,1,128]{3,2,1,0:T(1,128)}), f32[64,9,1,128]{3,2,1,0:T(1,128)S(1)}, u32[]{:S(2)}, u32[]{:S(2)}) async-start(f32[64,9,1,128]{3,2,1,0:T(1,128)} %bitcast.22), calls=%async_computation.2 | async-start | bytes 589824 | tf_op jit(solution)/shard_map/all_to_all | solution.py:465
